TPU v7x, 32 devices: a whole 2x2x4 slice. The times are simulated.
32 devices in a mesh: dp: 16 (over z, x, core), tensor: 2 (over y).
Axes of the slice: x: 2, y: 2, z: 4, core: 2. Of those that a mesh axis runs over, the one named last changes fastest.
Arguments:
- grad_hidden: bfloat16 [2048, 14336], P('dp', 'tensor'), may hold values from -18 to 18
- gate: bfloat16 [2048, 14336], P('dp', 'tensor'), may hold values from -6 to 6
Outputs:
- factor: float32 [14336, 14336], P('tensor', 'dp')
All inputs are finite; a program needn't handle non-finite values.
Results may differ from a plain program's by a relative error of at most 0.0065.
Values may be sent and summed in bfloat16 or wider, within the bound.
A program may use at most 128 MiB of HBM per device.

v0:
```python
import jax
import jax.numpy as jnp
from jax import lax
from jax.sharding import PartitionSpec as P

FF = 14336


def shards(grad_hidden, gate):
    up_grad = (grad_hidden.astype(jnp.float32) * jax.nn.silu(gate.astype(jnp.float32))).astype(
        jnp.bfloat16
    )
    tensor_count = lax.axis_size("tensor")
    data_count = lax.axis_size("dp")
    col_width = FF // data_count
    ratio = data_count // tensor_count
    data_index = lax.axis_index("dp")
    owner = data_index // ratio
    offset = data_index % ratio * col_width
    contract = (((0,), (0,)), ((), ()))
    total_tokens = up_grad.shape[0] * data_count
    rows_all = lax.all_gather(up_grad, "dp", axis=0, tiled=True)
    panel = lax.dynamic_slice_in_dim(rows_all, offset, col_width, 1)
    slices = lax.all_gather(panel, "tensor", axis=1, tiled=True)
    cols_all = lax.dynamic_slice_in_dim(slices, owner * col_width, col_width, 1)
    summed = lax.dot_general(rows_all, cols_all, contract, preferred_element_type=jnp.float32)
    return summed / total_tokens


def solution(mesh):
    return jax.shard_map(
        shards,
        mesh=mesh,
        in_specs=(P("dp", "tensor"), P("dp", "tensor")),
        out_specs=P("tensor", "dp"),
        check_vma=False,
    )
```

profile of v0, /device:TPU:27, one launch (start us, length us, event | category | flops | bytes accessed | tf_op | source)
XLA Modules:
  0.0 301.8 jit_solution(14807854129925651823)
XLA Ops:
  6.5 0.0 all-gather.3.cloned.1.call-start
  6.5 4.4 %fusion.5 = bf16[128,7168]{1,0:T(8,128)(2,1)} fusion(bf16[128,7168]{1,0:T(8,128)(2,1)} %param.3, bf16[128,7168]{1,0:T(8,128)(2,1)} %param.2), kind=kLoop, calls=%fused_computation.8 | loop fusion | flops 7340032 | bytes 5505024 | tf_op jit(solution)/shard_map/convert_element_type | solution.py:10
  10.9 0.0 all-gather.3.cloned.1.call-update
  11.0 0.0 all-gather.5.cloned.1.call-start
  11.0 148.8 %all-gather.3.cloned.1.call-done = bf16[2048,7168]{1,0:T(8,128)(2,1)} async-done(((bf16[128,7168]{1,0:T(8,128)(2,1)}), bf16[2048,7168]{1,0:T(8,128)(2,1)}) %all-gather.3.cloned.1.call-update) | async-done | bytes 29360144 | tf_op jit(solution)/shard_map/all_gather | solution.py:22
  159.8 4.2 %constant_dynamic-slice_fusion = bf16[2048,896]{1,0:T(8,128)(2,1)} fusion(bf16[2048,7168]{1,0:T(8,128)(2,1)} %all-gather.3.cloned.1.call-done, s32[]{:T(128)S(6)} %select_n.18), kind=kLoop, calls=%fused_computation.10 | loop fusion | bytes 7340036 | tf_op jit(solution)/shard_map/dynamic_slice | solution.py:23
  164.0 0.0 all-gather.5.cloned.1.call-update
  164.0 92.7 %all-gather.5.cloned.1.call-done = bf16[2048,1792]{1,0:T(8,128)(2,1)} async-done(((bf16[2048,896]{1,0:T(8,128)(2,1)}), bf16[2048,1792]{1,0:T(8,128)(2,1)}) %all-gather.5.cloned.1.call-update) | async-done | bytes 7340048 | tf_op jit(solution)/shard_map/all_gather | solution.py:24
  256.7 38.3 %convolution_multiply_fusion = f32[7168,896]{1,0:T(8,128)} fusion(bf16[2048,7168]{1,0:T(8,128)(2,1)} %all-gather.3.cloned.1.call-done, bf16[2048,1792]{1,0:T(8,128)(2,1)} %all-gather.5.cloned.1.call-done, s32[]{:T(128)S(6)} %select_n.20), kind=kOutput, calls=%fused_computation | convolution fusion | flops 26313097216 | bytes 58720260 | tf_op jit(solution)/shard_map/dot_general | solution.py:26
Async XLA Ops:
  6.5 153.3 %all-gather.3.cloned.1.call-start = ((), (), s32[]{:S(2)}) async-start(), calls=%async_computation | async-start | bytes 31195136 | tf_op jit(solution)/shard_map/all_gather | solution.py:22
  11.0 245.7 %all-gather.5.cloned.1.call-start = ((), (), s32[]{:S(2)}) async-start(), calls=%async_computation.1 | async-start | bytes 11010048 | tf_op jit(solution)/shard_map/all_gather | solution.py:24
Sparse Core Ops, SparseCore 0:
  11.1 148.6 all-gather.2
  164.1 92.5 all-gather.4
where the time goes:
time: 304 us; the launch traced here: 302 us
  waiting for transfers between devices  241 us (79%)
  matrix products  38.3 us (13%)
  between operations  13.4 us (4%)
  other arithmetic  4.39 us (1%)
  local copies, waits for them, and re-layouts  4.17 us (1%)
    all_gather x1, waiting for transfers between devices, shards(): rows_all = lax.all_gather(up_grad, 'dp', axis=0, tiled=True)  149 us
    all_gather x1, waiting for transfers between devices, shards(): slices = lax.all_gather(panel, 'tensor', axis=1, tiled=True)  92.7 us
    dot_general x1, matrix products, shards(): lax.dot_general(rows_all, cols_all, contract, preferred_element_type=jnp....  38.3 us
  transfers between devices with their start and end apart: 2, of which 2 were waited for; matrix products, arithmetic and copies ran while one was open for 0% of the time, Pallas kernels for 0%

commit v1 on v0

--- a/solution.py
+++ b/solution.py
@@ -1,18 +1,27 @@
+import functools
+
 import jax
 import jax.numpy as jnp
 from jax import lax
+from jax.experimental import pallas as pl
+from jax.experimental.pallas import tpu as pltpu
 from jax.sharding import PartitionSpec as P
 
-FF = 14336
-
-
-def shards(grad_hidden, gate):
-    up_grad = (grad_hidden.astype(jnp.float32) * jax.nn.silu(gate.astype(jnp.float32))).astype(
+MESH = pl.DeviceIdType.MESH
+LANES = 128
+
+
+def activations(grad_hidden, gate):
+    return (grad_hidden.astype(jnp.float32) * jax.nn.silu(gate.astype(jnp.float32))).astype(
         jnp.bfloat16
     )
+
+
+def plain(grad_hidden, gate):
+    up_grad = activations(grad_hidden, gate)
     tensor_count = lax.axis_size("tensor")
     data_count = lax.axis_size("dp")
-    col_width = FF // data_count
+    col_width = up_grad.shape[1] * tensor_count // data_count
     ratio = data_count // tensor_count
     data_index = lax.axis_index("dp")
     owner = data_index // ratio
@@ -27,6 +36,279 @@
     return summed / total_tokens
 
 
+def flip_kernel(g_ref, v_ref, o_ref):
+    v = v_ref[...].astype(jnp.float32)
+    u = g_ref[...].astype(jnp.float32) * (v / (1.0 + jnp.exp(-v)))
+    o_ref[...] = u.astype(jnp.bfloat16).T
+
+
+def flip(grad_hidden, gate, width):
+    tokens, hidden = grad_hidden.shape
+    return pl.pallas_call(
+        flip_kernel,
+        grid=(hidden // width,),
+        in_specs=[pl.BlockSpec((tokens, width), lambda i: (0, i))] * 2,
+        out_specs=pl.BlockSpec((width, tokens), lambda i: (i, 0)),
+        out_shape=jax.ShapeDtypeStruct((hidden, tokens), jnp.bfloat16),
+    )(grad_hidden, gate)
+
+
+def gather_kernel(dims, own_ref, all_ref, panel_ref, own_sem, z_send, x_send, c_send, y_send, recv, c_recv, y_recv):
+    line, count, cross, rows = dims
+    first = count - cross
+    me, t = lax.axis_index("dp"), lax.axis_index("tensor")
+    z, x, core = me // 4, me // 2 % 2, me % 2
+    chips = 2 * line
+    at = lambda zz, xx: zz * 2 + xx
+    here = at(z, x)
+    owns = (here // (chips // 2)) == t
+    part = here % (chips // 2)
+    per = count // (chips // 2)
+
+    up = (jnp.minimum(z + 1, line - 1) * 4 + x * 2 + core, t)
+    down = (jnp.maximum(z - 1, 0) * 4 + x * 2 + core, t)
+    over = (z * 4 + (1 - x) * 2 + core, t)
+    twin = (z * 4 + x * 2 + 1 - core, t)
+    has_up, has_down = z < line - 1, z > 0
+
+    barrier = pltpu.get_barrier_semaphore()
+    greet = lambda dev: pl.semaphore_signal(barrier, inc=1, device_id=dev, device_id_type=MESH)
+    greet(over)
+    greet(twin)
+    greet((me, 1 - t))
+    greet(twin[:1] + (1 - t,))
+    pl.when(has_up)(lambda: greet(up))
+    pl.when(has_down)(lambda: greet(down))
+    end = (z == 0) | (z == line - 1)
+    pl.semaphore_wait(barrier, jnp.where(end, 5, 6))
+
+    def rows_of(k):
+        return pl.ds(pl.multiple_of(k * rows, rows), rows)
+
+    def lanes_of(q):
+        return pl.ds(pl.multiple_of((q * 2 + core) * LANES, LANES), LANES)
+
+    def place(q, k):
+        return all_ref.at[rows_of(k), lanes_of(q)]
+
+    def source(q, k, own):
+        return own_ref.at[rows_of(k)] if own else place(q, k)
+
+    def along(q, k, way, own=False):
+        return pltpu.make_async_remote_copy(
+            src_ref=source(q, k, own), dst_ref=place(q, k), send_sem=z_send.at[way, q, k],
+            recv_sem=recv.at[q, k], device_id=(down, up)[way], device_id_type=MESH)
+
+    def across(q, k, own=False):
+        return pltpu.make_async_remote_copy(
+            src_ref=source(q, k, own), dst_ref=place(q, k), send_sem=x_send.at[q, k],
+            recv_sem=recv.at[q, k], device_id=over, device_id_type=MESH)
+
+    def to_twin(q, k, own=False):
+        return pltpu.make_async_remote_copy(
+            src_ref=source(q, k, own), dst_ref=place(q, k), send_sem=c_send.at[q, k],
+            recv_sem=c_recv.at[q, k], device_id=twin, device_id_type=MESH)
+
+    def to_panel(q, k, own=False):
+        j = k % per
+        half = per // 2
+        return pltpu.make_async_remote_copy(
+            src_ref=source(q, k, own),
+            dst_ref=panel_ref.at[rows_of(j % half), lanes_of(q)],
+            send_sem=y_send.at[q, j], recv_sem=y_recv.at[q * 2 + core, j % half],
+            device_id=(here * 2 + j // half, 1 - t), device_id_type=MESH)
+
+    def spread(q, k, own=False):
+        to_twin(q, k, own).start()
+        pl.when(owns & (k // per == part))(lambda: to_panel(q, k, own).start())
+
+    def arrive(q, k):
+        across(q, k).wait_recv()
+
+    keep = pltpu.make_async_copy(own_ref, all_ref.at[:, lanes_of(here)], own_sem)
+
+    @pl.loop(0, count)
+    def _(k):
+        pl.when(has_up)(lambda: along(here, k, 1, True).start())
+        pl.when(has_down)(lambda: along(here, k, 0, True).start())
+        across(here, k, True).start()
+        spread(here, k, True)
+
+    keep.start()
+
+    def from_line(s, k, way):
+        zz = z - s if way else z + s
+        valid = (zz >= 0) & (zz < line)
+
+        @pl.when(valid)
+        def _():
+            q = at(zz, x)
+            arrive(q, k)
+            pl.when(has_up if way else has_down)(lambda: along(q, k, way).start())
+            pl.when(k < first)(lambda: across(q, k).start())
+            spread(q, k)
+
+    def from_cross(s, k, way):
+        zz = z - s if way else z + s
+        valid = (zz >= 0) & (zz < line)
+
+        @pl.when(valid)
+        def _():
+            q = at(zz, 1 - x)
+            arrive(q, k)
+            pl.when(has_up if way else has_down)(lambda: along(q, k, way).start())
+            spread(q, k)
+
+    def relayed(s, k):
+        for zz in (z - s, z + s):
+            @pl.when((zz >= 0) & (zz < line))
+            def _():
+                q = at(zz, 1 - x)
+                arrive(q, k)
+                spread(q, k)
+
+    for s in range(1, line + 2):
+        @pl.loop(0, count)
+        def _(k):
+            if s < line:
+                from_line(s, k, 1)
+                from_line(s, k, 0)
+            if s == 1:
+                q = at(z, 1 - x)
+                arrive(q, k)
+                spread(q, k)
+            else:
+                @pl.when(k < first)
+                def _():
+                    if s - 1 < line:
+                        pl.when(end)(lambda: relayed(s - 1, k))
+                    if 1 <= s - 2 < line:
+                        pl.when(jnp.logical_not(end))(lambda: relayed(s - 2, k))
+
+        if s <= line:
+            @pl.loop(first, count)
+            def _(k):
+                if s == 1:
+                    q = at(z, 1 - x)
+                    pl.when(has_up)(lambda: along(q, k, 1).start())
+                    pl.when(has_down)(lambda: along(q, k, 0).start())
+                else:
+                    from_cross(s - 1, k, 1)
+                    from_cross(s - 1, k, 0)
+
+    keep.wait()
+
+    @pl.loop(0, chips)
+    def _(q):
+        zz, xx = q // 2, q % 2
+
+        @pl.loop(0, count)
+        def _(k):
+            to_twin(q, k).wait()
+            mine = xx == x
+            pl.when((mine | (zz == z)) & ((k < first) | (zz == z)) & mine)(lambda: across(q, k).wait_send())
+            goes = mine | (k >= first)
+            pl.when(goes & has_up & (zz <= z))(lambda: along(q, k, 1).wait_send())
+            pl.when(goes & has_down & (zz >= z))(lambda: along(q, k, 0).wait_send())
+            pl.when(owns & (k // per == part))(lambda: to_panel(q, k).wait_send())
+
+        @pl.loop(0, per // 2)
+        def _(j):
+            @pl.when(jnp.logical_not(owns))
+            def _():
+                for c in range(2):
+                    piece = panel_ref.at[rows_of(j), pl.ds(pl.multiple_of((q * 2 + c) * LANES, LANES), LANES)]
+                    pltpu.make_async_copy(piece, piece, y_recv.at[q * 2 + c, j]).wait()
+
+
+def gather(own, dims, width, tokens):
+    line, count, cross, rows = dims
+    chips = 2 * line
+    per = count // line
+    sem = pltpu.SemaphoreType.DMA
+    hidden = own.shape[0]
+    return pl.pallas_call(
+        functools.partial(gather_kernel, dims),
+        out_shape=(
+            jax.ShapeDtypeStruct((hidden, tokens), jnp.bfloat16),
+            jax.ShapeDtypeStruct((width, tokens), jnp.bfloat16),
+        ),
+        in_specs=[pl.BlockSpec(memory_space=pl.ANY)],
+        out_specs=(pl.BlockSpec(memory_space=pl.ANY),) * 2,
+        scratch_shapes=[
+            sem(()),
+            sem((2, chips, count)),
+            sem((chips, count)),
+            sem((chips, count)),
+            sem((chips, per)),
+            sem((chips, count)),
+            sem((chips, count)),
+            sem((2 * chips, per // 2)),
+        ],
+        compiler_params=pltpu.CompilerParams(collective_id=0, has_side_effects=True),
+    )(own)
+
+
+def matmul_kernel(total, width, a_ref, all_ref, panel_ref, o_ref, b_ref, sem):
+    me, t = lax.axis_index("dp"), lax.axis_index("tensor")
+    ratio = lax.axis_size("dp") // lax.axis_size("tensor")
+
+    @pl.when(pl.program_id(0) == 0)
+    def _():
+        owns = me // ratio == t
+
+        @pl.when(owns)
+        def _():
+            rows = pl.ds(pl.multiple_of(me % ratio * width, LANES), width)
+            pltpu.async_copy(all_ref.at[rows], b_ref, sem).wait()
+
+        @pl.when(jnp.logical_not(owns))
+        def _():
+            pltpu.async_copy(panel_ref, b_ref, sem).wait()
+
+    o_ref[...] = lax.dot_general(
+        a_ref[...], b_ref[...], (((1,), (1,)), ((), ())), preferred_element_type=jnp.float32
+    ) * (1.0 / total)
+
+
+def matmul(everything, panel, tile):
+    hidden, tokens = everything.shape
+    width = panel.shape[0]
+    return pl.pallas_call(
+        functools.partial(matmul_kernel, tokens, width),
+        grid=(hidden // tile,),
+        in_specs=[
+            pl.BlockSpec((tile, tokens), lambda i: (i, 0)),
+            pl.BlockSpec(memory_space=pl.ANY),
+            pl.BlockSpec(memory_space=pl.ANY),
+        ],
+        out_specs=pl.BlockSpec((tile, width), lambda i: (i, 0)),
+        out_shape=jax.ShapeDtypeStruct((hidden, width), jnp.float32),
+        scratch_shapes=[pltpu.VMEM((width, tokens), jnp.bfloat16), pltpu.SemaphoreType.DMA(())],
+        compiler_params=pltpu.CompilerParams(vmem_limit_bytes=48 * 2**20),
+    )(everything, everything, panel)
+
+
+def shards(grad_hidden, gate):
+    tensor_count, data_count = lax.axis_size("tensor"), lax.axis_size("dp")
+    mine, hidden = grad_hidden.shape
+    width = hidden * tensor_count // data_count
+    tokens = mine * data_count
+    count = data_count
+    fits = (
+        tensor_count == 2 and data_count % 4 == 0 and data_count > 4 and mine == LANES and width % LANES == 0
+        and hidden % (16 * count) == 0 and tokens & (tokens - 1) == 0 and hidden % 1024 == 0
+    )
+    if not fits:
+        return plain(grad_hidden, gate)
+    line = data_count // 4
+    cross = round(count / (2 * (line - 1)))
+    dims = (line, count, cross, hidden // count)
+    own = flip(grad_hidden, gate, 1024)
+    everything, panel = gather(own, dims, width, tokens)
+    return matmul(everything, panel, 1024)
+
+
 def solution(mesh):
     return jax.shard_map(
         shards,

time: 304 us -> 208 us (0.68)
  waiting for transfers between devices: 241 us -> 0 us
  Pallas kernels: 0 us -> 205 us
  matrix products: 38.3 us -> 0 us
  between operations: 13.4 us -> 0.02 us
  other arithmetic: 4.39 us -> 0 us
    all_gather x2 -> x0, waiting for transfers between devices: 241 us -> none  [the longest x1 149 us: shards(): rows_all = lax.all_gather(up_grad, 'dp', axis=0, tiled=True)]
    pallas_call x0 -> x3, Pallas kernels: none -> 205 us  [the longest x1 163 us: gather(): pl.pallas_call(functools.partial(gather_kernel, dims), out_shape=(jax.Sha...]
    dot_general x1 -> x0, matrix products: 38.3 us -> none  [shards(): lax.dot_general(rows_all, cols_all, contract, preferred_element_type=jnp....]
    convert_element_type x1 -> x0, other arithmetic: 4.39 us -> none  [shards(): (grad_hidden.astype(jnp.float32) * jax.nn.silu(gate.astype(jnp.float32)))...]
    dynamic_slice x1 -> x0, local copies, waits for them, and re-layouts: 4.17 us -> none  [shards(): panel = lax.dynamic_slice_in_dim(rows_all, offset, col_width, 1)]
  transfers between devices with their start and end apart: 2 -> 0, of which waited for: 2 -> 0; matrix products, arithmetic and copies ran while one was open for 0% -> 0% of each run, Pallas kernels for 0% -> 0%
where the time goes in v1:
time: 208 us; the launch traced here: 207 us
  Pallas kernels  205 us (99%)
    pallas_call x1, Pallas kernels, gather(): pl.pallas_call(functools.partial(gather_kernel, dims), out_shape=(jax.Sha...  163 us
    pallas_call x1, Pallas kernels, matmul(): pl.pallas_call(functools.partial(matmul_kernel, tokens, width), grid=(hid...  36.1 us
    pallas_call x1, Pallas kernels, flip(): pl.pallas_call(flip_kernel, grid=(hidden // width,), in_specs=[pl.BlockSp...  6.14 us

profile of v1, /device:TPU:27, one launch (start us, length us, event | category | flops | bytes accessed | tf_op | source)
XLA Modules:
  0.0 207.1 jit_solution(4660004501338615517)
XLA Ops:
  0.0 6.1 %shard_map.28.own_ref = bf16[7168,128]{1,0:T(8,128)(2,1)} custom-call(bf16[128,7168]{1,0:T(8,128)(2,1)} %g_ref.1, bf16[128,7168]{1,0:T(8,128)(2,1)} %v_ref.1), custom_call_target="tpu_custom_call" | custom-call | tf_op jit(solution)/shard_map/pallas_call | solution.py:47
  6.1 162.8 %shard_map.29 = (bf16[7168,2048]{1,0:T(8,128)(2,1)}, bf16[896,2048]{1,0:T(8,128)(2,1)}) custom-call(bf16[7168,128]{1,0:T(8,128)(2,1)} %shard_map.28.own_ref), custom_call_target="tpu_custom_call" | custom-call | tf_op jit(solution)/shard_map/pallas_call | solution.py:230
  169.0 0.0 copy-start
  169.0 2.0 copy-done
  171.0 36.1 %shard_map.30 = f32[7168,896]{1,0:T(8,128)} custom-call(bf16[7168,2048]{1,0:T(8,128)(2,1)} %get-tuple-element.7.a_ref.all_ref, bf16[7168,2048]{1,0:T(8,128)(2,1)} %get-tuple-element.7.a_ref.all_ref, bf16[896,2048]{1,0:T(8,128)(2,1)S(1)} %copy-done), custom_call_target="tpu_custom_call" | custom-call | tf_op jit(solution)/shard_map/pallas_call | solution.py:277
Async XLA Ops:
  169.0 2.0 copy-start

commit v2 on v1

--- a/solution.py
+++ b/solution.py
@@ -53,7 +53,26 @@
     )(grad_hidden, gate)
 
 
-def gather_kernel(dims, own_ref, all_ref, panel_ref, own_sem, z_send, x_send, c_send, y_send, recv, c_recv, y_recv):
+def early(line, z, x):
+    near = jnp.where(z == 0, 1, z - 1)
+    next_near = jnp.where(z == 0, 2, jnp.where(z == line - 1, line - 3, z + 1))
+    return [z * 2 + x, z * 2 + 1 - x, near * 2 + x, next_near * 2 + x]
+
+
+def late(line, z, x):
+    low = jnp.where(z == 0, 0, jnp.where(z == line - 1, line - 3, z - 1))
+    rest = [(i + jnp.where(i >= low, 3, 0)) * 2 + x for i in range(line - 3)]
+    return rest + [(i + jnp.where(i >= z, 1, 0)) * 2 + 1 - x for i in range(line - 1)]
+
+
+def nt_dot(a, b):
+    return lax.dot_general(a, b, (((1,), (1,)), ((), ())), preferred_element_type=jnp.float32)
+
+
+def gather_kernel(
+    dims, own_ref, all_ref, panel_ref, part_ref, own_sem, z_send, x_send, c_send, y_send,
+    recv, c_recv, y_recv, a_ref, b_ref, a_sem, b_sem,
+):
     line, count, cross, rows = dims
     first = count - cross
     me, t = lax.axis_index("dp"), lax.axis_index("tensor")
@@ -167,9 +186,77 @@
                 arrive(q, k)
                 spread(q, k)
 
+    def pair_of(q):
+        return pl.ds(pl.multiple_of(q * 2 * LANES, 2 * LANES), 2 * LANES)
+
+    def slab(j):
+        return pl.ds(j * 2 * LANES, 2 * LANES)
+
+    chosen = early(line, z, x)
+
+    def tile_copies(k, slot):
+        return [
+            pltpu.make_async_copy(
+                all_ref.at[rows_of(k), pair_of(q)], a_ref.at[slot, :, slab(j)], a_sem.at[slot, j]
+            )
+            for j, q in enumerate(chosen)
+        ]
+
+    def prepare():
+        keep.wait()
+        for q in chosen:
+            @pl.loop(0, count)
+            def _(k):
+                to_twin(q, k).wait_recv()
+            panel_arrived(q)
+        for tile in tile_copies(0, 0):
+            tile.start()
+        for ours in (True, False):
+            @pl.when(owns == ours)
+            def _():
+                width = rows * per // 2
+                from_ref = (
+                    all_ref.at[pl.ds(pl.multiple_of((part * 2 + core) * width, width), width)]
+                    if ours else panel_ref
+                )
+                copies = [
+                    pltpu.make_async_copy(from_ref.at[:, pair_of(q)], b_ref.at[:, slab(j)], b_sem.at[j])
+                    for j, q in enumerate(chosen)
+                ]
+                for copy in copies:
+                    copy.start()
+                for copy in copies:
+                    copy.wait()
+
+    def multiply(k):
+        slot = k % 2
+
+        @pl.when(k + 1 < count)
+        def _():
+            for tile in tile_copies(k + 1, 1 - slot):
+                tile.start()
+
+        for tile in tile_copies(k, slot):
+            tile.wait()
+        part_ref[rows_of(k), :] = nt_dot(a_ref[slot], b_ref[...])
+
+    def panel_arrived(q):
+        @pl.when(jnp.logical_not(owns))
+        def _():
+            @pl.loop(0, per // 2)
+            def _(j):
+                for c in range(2):
+                    piece = panel_ref.at[rows_of(j), pl.ds(pl.multiple_of((q * 2 + c) * LANES, LANES), LANES)]
+                    pltpu.make_async_copy(piece, piece, y_recv.at[q * 2 + c, j]).wait()
+
     for s in range(1, line + 2):
+        if s == 3:
+            prepare()
+
         @pl.loop(0, count)
         def _(k):
+            if s == 3:
+                multiply(k)
             if s < line:
                 from_line(s, k, 1)
                 from_line(s, k, 0)
@@ -196,29 +283,24 @@
                     from_cross(s - 1, k, 1)
                     from_cross(s - 1, k, 0)
 
-    keep.wait()
+    for q in late(line, z, x):
+        @pl.loop(0, count)
+        def _(k):
+            to_twin(q, k).wait_recv()
+        panel_arrived(q)
 
     @pl.loop(0, chips)
     def _(q):
-        zz, xx = q // 2, q % 2
+        zz, mine = q // 2, q % 2 == x
 
         @pl.loop(0, count)
         def _(k):
-            to_twin(q, k).wait()
-            mine = xx == x
-            pl.when((mine | (zz == z)) & ((k < first) | (zz == z)) & mine)(lambda: across(q, k).wait_send())
+            to_twin(q, k).wait_send()
+            pl.when(mine & ((k < first) | (zz == z)))(lambda: across(q, k).wait_send())
             goes = mine | (k >= first)
             pl.when(goes & has_up & (zz <= z))(lambda: along(q, k, 1).wait_send())
             pl.when(goes & has_down & (zz >= z))(lambda: along(q, k, 0).wait_send())
             pl.when(owns & (k // per == part))(lambda: to_panel(q, k).wait_send())
-
-        @pl.loop(0, per // 2)
-        def _(j):
-            @pl.when(jnp.logical_not(owns))
-            def _():
-                for c in range(2):
-                    piece = panel_ref.at[rows_of(j), pl.ds(pl.multiple_of((q * 2 + c) * LANES, LANES), LANES)]
-                    pltpu.make_async_copy(piece, piece, y_recv.at[q * 2 + c, j]).wait()
 
 
 def gather(own, dims, width, tokens):
@@ -232,9 +314,14 @@
         out_shape=(
             jax.ShapeDtypeStruct((hidden, tokens), jnp.bfloat16),
             jax.ShapeDtypeStruct((width, tokens), jnp.bfloat16),
+            pltpu.VMEM((hidden, width), jnp.float32),
         ),
         in_specs=[pl.BlockSpec(memory_space=pl.ANY)],
-        out_specs=(pl.BlockSpec(memory_space=pl.ANY),) * 2,
+        out_specs=(
+            pl.BlockSpec(memory_space=pl.ANY),
+            pl.BlockSpec(memory_space=pl.ANY),
+            pl.BlockSpec(memory_space=pltpu.VMEM),
+        ),
         scratch_shapes=[
             sem(()),
             sem((2, chips, count)),
@@ -244,49 +331,78 @@
             sem((chips, count)),
             sem((chips, count)),
             sem((2 * chips, per // 2)),
+            pltpu.VMEM((2, rows, 8 * LANES), jnp.bfloat16),
+            pltpu.VMEM((width, 8 * LANES), jnp.bfloat16),
+            sem((2, 4)),
+            sem((4,)),
         ],
-        compiler_params=pltpu.CompilerParams(collective_id=0, has_side_effects=True),
+        compiler_params=pltpu.CompilerParams(
+            collective_id=0, has_side_effects=True, vmem_limit_bytes=36 * 2**20
+        ),
     )(own)
 
 
-def matmul_kernel(total, width, a_ref, all_ref, panel_ref, o_ref, b_ref, sem):
+def matmul_kernel(total, width, left, chips_ref, *refs):
+    pieces, (all_ref, panel_ref, part_ref, o_ref, b_ref, sem) = refs[:left], refs[left:]
     me, t = lax.axis_index("dp"), lax.axis_index("tensor")
     ratio = lax.axis_size("dp") // lax.axis_size("tensor")
-
-    @pl.when(pl.program_id(0) == 0)
+    step, tile = pl.program_id(0), o_ref.shape[0]
+
+    @pl.when(step == 0)
     def _():
-        owns = me // ratio == t
-
-        @pl.when(owns)
-        def _():
-            rows = pl.ds(pl.multiple_of(me % ratio * width, LANES), width)
-            pltpu.async_copy(all_ref.at[rows], b_ref, sem).wait()
-
-        @pl.when(jnp.logical_not(owns))
-        def _():
-            pltpu.async_copy(panel_ref, b_ref, sem).wait()
-
-    o_ref[...] = lax.dot_general(
-        a_ref[...], b_ref[...], (((1,), (1,)), ((), ())), preferred_element_type=jnp.float32
-    ) * (1.0 / total)
-
-
-def matmul(everything, panel, tile):
+        for ours in (True, False):
+            @pl.when((me // ratio == t) == ours)
+            def _():
+                rows = pl.ds(pl.multiple_of(me % ratio * width, LANES), width)
+                from_ref = all_ref.at[rows] if ours else panel_ref
+                copies = [
+                    pltpu.make_async_copy(
+                        from_ref.at[:, pl.ds(pl.multiple_of(chips_ref[j] * 2 * LANES, LANES), 2 * LANES)],
+                        b_ref.at[:, pl.ds(j * 2 * LANES, 2 * LANES)],
+                        sem.at[j],
+                    )
+                    for j in range(left)
+                ]
+                for copy in copies:
+                    copy.start()
+                for copy in copies:
+                    copy.wait()
+
+    a = jnp.concatenate([piece[...] for piece in pieces], axis=1)
+    done = part_ref[pl.ds(pl.multiple_of(step * tile, tile), tile), :]
+    o_ref[...] = (done + nt_dot(a, b_ref[...])) * (1.0 / total)
+
+
+def matmul(everything, panel, part, chips, tile):
     hidden, tokens = everything.shape
     width = panel.shape[0]
+    left = chips.shape[0]
+    everything = pltpu.with_memory_space_constraint(everything, pltpu.HBM)
+    panel = pltpu.with_memory_space_constraint(panel, pltpu.HBM)
+    part = pltpu.with_memory_space_constraint(part, pltpu.VMEM)
+
+    def piece(j):
+        return pl.BlockSpec((tile, 2 * LANES), lambda i, chips_ref: (i, chips_ref[j]))
+
     return pl.pallas_call(
-        functools.partial(matmul_kernel, tokens, width),
-        grid=(hidden // tile,),
-        in_specs=[
-            pl.BlockSpec((tile, tokens), lambda i: (i, 0)),
-            pl.BlockSpec(memory_space=pl.ANY),
-            pl.BlockSpec(memory_space=pl.ANY),
-        ],
-        out_specs=pl.BlockSpec((tile, width), lambda i: (i, 0)),
+        functools.partial(matmul_kernel, tokens, width, left),
+        grid_spec=pltpu.PrefetchScalarGridSpec(
+            num_scalar_prefetch=1,
+            grid=(hidden // tile,),
+            in_specs=[piece(j) for j in range(left)] + [
+                pl.BlockSpec(memory_space=pltpu.HBM),
+                pl.BlockSpec(memory_space=pltpu.HBM),
+                pl.BlockSpec(memory_space=pltpu.VMEM),
+            ],
+            out_specs=pl.BlockSpec((tile, width), lambda i, chips_ref: (i, 0)),
+            scratch_shapes=[
+                pltpu.VMEM((width, left * 2 * LANES), jnp.bfloat16),
+                pltpu.SemaphoreType.DMA((left,)),
+            ],
+        ),
         out_shape=jax.ShapeDtypeStruct((hidden, width), jnp.float32),
-        scratch_shapes=[pltpu.VMEM((width, tokens), jnp.bfloat16), pltpu.SemaphoreType.DMA(())],
-        compiler_params=pltpu.CompilerParams(vmem_limit_bytes=48 * 2**20),
-    )(everything, everything, panel)
+        compiler_params=pltpu.CompilerParams(vmem_limit_bytes=36 * 2**20),
+    )(chips, *[everything] * (left + 1), panel, part)
 
 
 def shards(grad_hidden, gate):
@@ -296,7 +412,7 @@
     tokens = mine * data_count
     count = data_count
     fits = (
-        tensor_count == 2 and data_count % 4 == 0 and data_count > 4 and mine == LANES and width % LANES == 0
+        tensor_count == 2 and data_count % 4 == 0 and data_count >= 16 and mine == LANES and width % LANES == 0
         and hidden % (16 * count) == 0 and tokens & (tokens - 1) == 0 and hidden % 1024 == 0
     )
     if not fits:
@@ -305,8 +421,10 @@
     cross = round(count / (2 * (line - 1)))
     dims = (line, count, cross, hidden // count)
     own = flip(grad_hidden, gate, 1024)
-    everything, panel = gather(own, dims, width, tokens)
-    return matmul(everything, panel, 1024)
+    everything, panel, part = gather(own, dims, width, tokens)
+    index = lax.axis_index("dp")
+    chips = jnp.stack(late(line, index // 4, index // 2 % 2)).astype(jnp.int32)
+    return matmul(everything, panel, part, chips, 512)
 
 
 def solution(mesh):

time: 208 us -> 198 us (0.952)
  Pallas kernels: 205 us -> 196 us
    pallas_call x1, Pallas kernels: 36.1 us -> 26.6 us  [matmul(): pl.pallas_call(functools.partial(matmul_kernel, tokens, width, left), gri...]
where the time goes in v2:
time: 198 us; the launch traced here: 197 us
  Pallas kernels  196 us (99%)
    pallas_call x1, Pallas kernels, gather(): pl.pallas_call(functools.partial(gather_kernel, dims), out_shape=(jax.Sha...  163 us
    pallas_call x1, Pallas kernels, matmul(): pl.pallas_call(functools.partial(matmul_kernel, tokens, width, left), gri...  26.6 us
    pallas_call x1, Pallas kernels, flip(): pl.pallas_call(flip_kernel, grid=(hidden // width,), in_specs=[pl.BlockSp...  6.14 us

profile of v2, /device:TPU:27, one launch (start us, length us, event | category | flops | bytes accessed | tf_op | source)
XLA Modules:
  0.0 196.6 jit_solution(7864426991715761341)
XLA Ops:
  0.0 0.6 pad_add_fusion.chips_ref
  0.6 6.1 %shard_map.28.own_ref = bf16[7168,128]{1,0:T(8,128)(2,1)} custom-call(bf16[128,7168]{1,0:T(8,128)(2,1)} %g_ref.1, bf16[128,7168]{1,0:T(8,128)(2,1)} %v_ref.1), custom_call_target="tpu_custom_call" | custom-call | tf_op jit(solution)/shard_map/pallas_call | solution.py:47
  6.7 163.2 %shard_map.29 = (bf16[7168,2048]{1,0:T(8,128)(2,1)}, bf16[896,2048]{1,0:T(8,128)(2,1)}, f32[7168,896]{1,0:T(8,128)S(1)}) custom-call(bf16[7168,128]{1,0:T(8,128)(2,1)} %shard_map.28.own_ref), custom_call_target="tpu_custom_call" | custom-call | tf_op jit(solution)/shard_map/pallas_call | solution.py:312
  170.0 26.6 %shard_map.30 = f32[7168,896]{1,0:T(8,128)} custom-call(s32[4]{0:T(128)} %pad_add_fusion.chips_ref, bf16[7168,2048]{1,0:T(8,128)(2,1)} %get-tuple-element.8.refs_0_.refs_1_.refs_2_.refs_3_.refs_4_, bf16[7168,2048]{1,0:T(8,128)(2,1)} %get-tuple-element.8.refs_0_.refs_1_.refs_2_.refs_3_.refs_4_, ...), custom_call_target="tpu_custom_call" | custom-call | tf_op jit(solution)/shard_map/pallas_call | solution.py:387

commit v3 on v2

--- a/solution.py
+++ b/solution.py
@@ -54,15 +54,29 @@
 
 
 def early(line, z, x):
-    near = jnp.where(z == 0, 1, z - 1)
-    next_near = jnp.where(z == 0, 2, jnp.where(z == line - 1, line - 3, z + 1))
-    return [z * 2 + x, z * 2 + 1 - x, near * 2 + x, next_near * 2 + x]
+    end, low, high = (z == 0) | (z == line - 1), z == 0, z == line - 1
+    near = jnp.where(low, 1, z - 1)
+    after = jnp.where(low, 2, jnp.where(high, line - 3, z + 1))
+    inner = jnp.where(z < line - 2, z + 2, z - 2) * 2 + x
+    far = jnp.where(low, 3, line - 4) * 2 + x
+    other = near * 2 + 1 - x
+    five = [z * 2 + x, z * 2 + 1 - x, near * 2 + x, after * 2 + x, jnp.where(end, other, inner)]
+    return five + [jnp.where(end, far, other)]
+
+
+def member(q, chosen):
+    return functools.reduce(jnp.logical_or, [q == c for c in chosen])
 
 
 def late(line, z, x):
-    low = jnp.where(z == 0, 0, jnp.where(z == line - 1, line - 3, z - 1))
-    rest = [(i + jnp.where(i >= low, 3, 0)) * 2 + x for i in range(line - 3)]
-    return rest + [(i + jnp.where(i >= z, 1, 0)) * 2 + 1 - x for i in range(line - 1)]
+    chosen = early(line, z, x)
+    left = 2 * line - len(chosen)
+    picked, rank = [jnp.int32(0)] * left, jnp.int32(0)
+    for q in range(2 * line):
+        free = jnp.logical_not(member(q, chosen))
+        picked = [jnp.where(free & (rank == j), q, p) for j, p in enumerate(picked)]
+        rank = rank + free.astype(jnp.int32)
+    return picked
 
 
 def nt_dot(a, b):
@@ -193,23 +207,23 @@
         return pl.ds(j * 2 * LANES, 2 * LANES)
 
     chosen = early(line, z, x)
-
-    def tile_copies(k, slot):
+    first_group, second_group = chosen[:-1], chosen[-1:]
+
+    def tile_copies(group, k, slot):
         return [
             pltpu.make_async_copy(
                 all_ref.at[rows_of(k), pair_of(q)], a_ref.at[slot, :, slab(j)], a_sem.at[slot, j]
             )
-            for j, q in enumerate(chosen)
+            for j, q in enumerate(group)
         ]
 
-    def prepare():
-        keep.wait()
-        for q in chosen:
+    def prepare(group):
+        for q in group:
             @pl.loop(0, count)
             def _(k):
                 to_twin(q, k).wait_recv()
             panel_arrived(q)
-        for tile in tile_copies(0, 0):
+        for tile in tile_copies(group, 0, 0):
             tile.start()
         for ours in (True, False):
             @pl.when(owns == ours)
@@ -221,24 +235,28 @@
                 )
                 copies = [
                     pltpu.make_async_copy(from_ref.at[:, pair_of(q)], b_ref.at[:, slab(j)], b_sem.at[j])
-                    for j, q in enumerate(chosen)
+                    for j, q in enumerate(group)
                 ]
                 for copy in copies:
                     copy.start()
                 for copy in copies:
                     copy.wait()
 
-    def multiply(k):
+    def multiply(group, k, add):
         slot = k % 2
 
         @pl.when(k + 1 < count)
         def _():
-            for tile in tile_copies(k + 1, 1 - slot):
+            for tile in tile_copies(group, k + 1, 1 - slot):
                 tile.start()
 
-        for tile in tile_copies(k, slot):
+        for tile in tile_copies(group, k, slot):
             tile.wait()
-        part_ref[rows_of(k), :] = nt_dot(a_ref[slot], b_ref[...])
+        span = pl.ds(0, len(group) * 2 * LANES)
+        product = nt_dot(a_ref[slot, :, span], b_ref[:, span])
+        if add:
+            product += part_ref[rows_of(k), :]
+        part_ref[rows_of(k), :] = product
 
     def panel_arrived(q):
         @pl.when(jnp.logical_not(owns))
@@ -251,12 +269,17 @@
 
     for s in range(1, line + 2):
         if s == 3:
-            prepare()
+            keep.wait()
+            prepare(first_group)
+        if s == 4:
+            prepare(second_group)
 
         @pl.loop(0, count)
         def _(k):
             if s == 3:
-                multiply(k)
+                multiply(first_group, k, False)
+            if s == 4:
+                multiply(second_group, k, True)
             if s < line:
                 from_line(s, k, 1)
                 from_line(s, k, 0)
@@ -283,11 +306,14 @@
                     from_cross(s - 1, k, 1)
                     from_cross(s - 1, k, 0)
 
-    for q in late(line, z, x):
-        @pl.loop(0, count)
-        def _(k):
-            to_twin(q, k).wait_recv()
-        panel_arrived(q)
+    @pl.loop(0, chips)
+    def _(q):
+        @pl.when(jnp.logical_not(member(q, chosen)))
+        def _():
+            @pl.loop(0, count)
+            def _(k):
+                to_twin(q, k).wait_recv()
+            panel_arrived(q)
 
     @pl.loop(0, chips)
     def _(q):
@@ -331,10 +357,10 @@
             sem((chips, count)),
             sem((chips, count)),
             sem((2 * chips, per // 2)),
-            pltpu.VMEM((2, rows, 8 * LANES), jnp.bfloat16),
-            pltpu.VMEM((width, 8 * LANES), jnp.bfloat16),
-            sem((2, 4)),
-            sem((4,)),
+            pltpu.VMEM((2, rows, 10 * LANES), jnp.bfloat16),
+            pltpu.VMEM((width, 10 * LANES), jnp.bfloat16),
+            sem((2, 5)),
+            sem((5,)),
         ],
         compiler_params=pltpu.CompilerParams(
             collective_id=0, has_side_effects=True, vmem_limit_bytes=36 * 2**20

time: 198 us -> 197 us (level)
    pallas_call x1, Pallas kernels: 26.6 us -> 19.6 us  [matmul(): pl.pallas_call(functools.partial(matmul_kernel, tokens, width, left), gri...]
    pallas_call x1, Pallas kernels: 163 us -> 170 us  [gather(): pl.pallas_call(functools.partial(gather_kernel, dims), out_shape=(jax.Sha...]
where the time goes in v3:
time: 197 us; the launch traced here: 196 us
  Pallas kernels  196 us (99%)
    pallas_call x1, Pallas kernels, gather(): pl.pallas_call(functools.partial(gather_kernel, dims), out_shape=(jax.Sha...  170 us
    pallas_call x1, Pallas kernels, matmul(): pl.pallas_call(functools.partial(matmul_kernel, tokens, width, left), gri...  19.6 us
    pallas_call x1, Pallas kernels, flip(): pl.pallas_call(flip_kernel, grid=(hidden // width,), in_specs=[pl.BlockSp...  6.14 us

profile of v3, /device:TPU:27, one launch (start us, length us, event | category | flops | bytes accessed | tf_op | source)
XLA Modules:
  0.0 196.2 jit_solution(15371670837711345136)
XLA Ops:
  0.0 0.6 pad_add_fusion.chips_ref
  0.6 6.1 %shard_map.28.own_ref = bf16[7168,128]{1,0:T(8,128)(2,1)} custom-call(bf16[128,7168]{1,0:T(8,128)(2,1)} %g_ref.1, bf16[128,7168]{1,0:T(8,128)(2,1)} %v_ref.1), custom_call_target="tpu_custom_call" | custom-call | tf_op jit(solution)/shard_map/pallas_call | solution.py:47
  6.7 169.8 %shard_map.29 = (bf16[7168,2048]{1,0:T(8,128)(2,1)}, bf16[896,2048]{1,0:T(8,128)(2,1)}, f32[7168,896]{1,0:T(8,128)S(1)}) custom-call(bf16[7168,128]{1,0:T(8,128)(2,1)} %shard_map.28.own_ref), custom_call_target="tpu_custom_call" | custom-call | tf_op jit(solution)/shard_map/pallas_call | solution.py:338
  176.6 19.6 %shard_map.30 = f32[7168,896]{1,0:T(8,128)} custom-call(s32[2]{0:T(128)} %pad_add_fusion.chips_ref, bf16[7168,2048]{1,0:T(8,128)(2,1)} %get-tuple-element.8.refs_0_.refs_1_.refs_2_, bf16[7168,2048]{1,0:T(8,128)(2,1)} %get-tuple-element.8.refs_0_.refs_1_.refs_2_, bf16[7168,2048]{1,0:T(8,128)(2,1)} %get-tuple-element.8.refs_0_.refs_1_.refs_2_, ...), custom_call_target="tpu_custom_call" | custom-call | tf_op jit(solution)/shard_map/pallas_call | solution.py:413
